TPU v7x, 256 devices: a whole 4x4x8 slice. The times are simulated.
256 devices in a mesh: team: 8 (over x, core), row: 2 (over z_hi), col: 16 (over y, z_lo).
Axes of the slice: x: 4, y: 4, z: 8 (z_hi: 2, z_lo: 4; z = z_hi * 4 + z_lo), core: 2. Of those that a mesh axis runs over, the one named last changes fastest.
Arguments:
- old_tiles: bfloat16 [8, 768, 256, 256], P('team', ('row', 'col')), may hold values from -4 to 4
- remap: int32 [8, 768], P('team', ('row', 'col')), may hold values from 0 to 255, as said below
- pivot_cols: bfloat16 [8, 5120, 1024], P('team', ('row', 'col')), may hold values from -6 to 6
- pivot_order: int32 [8, 2, 512], P('team'), may hold values from 0 to 511, each once within a row
- pivot_pattern: int32 [8, 2, 256], P('team'), may hold values 0 or 1
- block_inverses: float32 [8, 2, 3, 256], P('team'), may hold values from -0.05 to 0.05
- delays: int32 [8, 2], P('team'), may hold values from 0 to 128
Outputs:
- parent: float32 [2, 2048, 4096], P('row', 'team', 'col')
- second_panel: float32 [8, 5120, 512], P('team', ('row', 'col'))
Inputs may be any that keep to these rules, and one draw needn't show every extreme that they name: `remap`: tiles that one device holds go to at most 12 distinct owners, the owner of tile (i, j) being the device at row i // 8, column j; at most 2 of one device's tiles go to one owner, and in every front some owner receives exactly 2 tiles from every device.
All inputs are finite; a program needn't handle non-finite values. No bound on the sum of `pivot_pattern` on one device may be relied on, other than what follows from the above.
Results may differ from a plain program's by a relative error of at most 0.0003.
Values may be sent and summed in bfloat16 or wider, within the bound.
A program may use at most 128 MiB of HBM per device.

v0:
```python
import jax
import jax.numpy as jnp
from jax import lax
from jax.sharding import Mesh
from jax.sharding import PartitionSpec as P

COL = ("col_0", "col_1")
ROW_COL = ("row", "col_0", "col_1")


def laid_out(pieces, dim):
    shape = list(pieces.shape[1:])
    shape[dim] *= pieces.shape[0]
    return jnp.moveaxis(pieces, 0, dim).reshape(shape)


def all_blocks(shard, axes, sequence):
    pieces = shard[None]
    for k in sequence:
        pieces = lax.all_gather(pieces, axes[k], axis=0, tiled=True)
    current = [lax.axis_size(axes[k]) for k in reversed(sequence)]
    pieces = pieces.reshape(*current, *shard.shape)
    turned = sorted(range(len(sequence)), key=lambda place: sequence[len(sequence) - 1 - place])
    return pieces.transpose(*turned, *range(len(sequence), pieces.ndim)).reshape(-1, *shard.shape)


def gather_axes(shard, axes, sequence, dim):
    return laid_out(all_blocks(shard, axes, sequence), dim)


def in_blocks(shard, dim, peers):
    before, after = (shard.shape[:dim], shard.shape[dim + 1 :])
    return jnp.moveaxis(shard.reshape(*before, peers, -1, *after), dim, 0)


def summed_on_arrival(shard, axis, dim):
    pieces = in_blocks(shard, dim, lax.axis_size(axis))
    arrived = lax.all_to_all(pieces, axis, split_axis=0, concat_axis=0, tiled=True)
    return arrived.sum(axis=0)


def make_coeffs(inverses, pattern, delay, panel):
    half_panel = panel // 2
    positions = jnp.arange(panel, dtype=jnp.int32)
    active = (positions < panel - delay).astype(jnp.float32)
    active_lo = active[:half_panel]
    active_hi = active[half_panel:]
    diag_one = inverses[0] * active_lo
    off_diag = inverses[1] * pattern.astype(jnp.float32) * active_lo * active_hi
    diag_two = inverses[2] * active_hi
    return (diag_one, off_diag, diag_two)


def scale_pivots(columns, coeffs):
    diag_one, off_diag, diag_two = coeffs
    half_panel = diag_one.shape[0]
    left_half = columns[:, :half_panel]
    right_half = columns[:, half_panel:]
    return jnp.concatenate(
        [
            left_half * diag_one + right_half * off_diag,
            left_half * off_diag + right_half * diag_two,
        ],
        axis=1,
    )


def outer_update(left_rows, right_rows):
    return lax.dot_general(
        left_rows,
        right_rows,
        (((1,), (1,)), ((), ())),
        precision=lax.Precision.HIGHEST,
        preferred_element_type=jnp.float32,
    )


def local(old_tiles, remap, pivot_cols, pivot_order, pivot_pattern, block_inverses, delays):
    row_devices = lax.axis_size("row")
    col_devices = lax.axis_size(COL)
    peers = row_devices * col_devices
    row_index = lax.axis_index("row")
    col_index = lax.axis_index(COL)
    held = old_tiles.shape[1]
    tile_side = old_tiles.shape[2]
    panel = pivot_order.shape[2]
    rows_here = pivot_cols.shape[1]
    front_order = rows_here * peers
    contrib = front_order - 2 * panel
    tile_count = contrib // tile_side
    row_span = contrib // row_devices
    col_span = contrib // col_devices
    per_row = row_span // tile_side
    per_col = col_span // tile_side
    old_flat = old_tiles[0].reshape(held, tile_side * tile_side)
    targets = remap[0]
    tile_row = targets // tile_count
    tile_col = targets % tile_count
    owners = tile_row // per_row * col_devices + tile_col // per_col
    slots = tile_row % per_row * per_col + tile_col % per_col
    spread = min(peers, held // 2)
    capacity = (held + spread - 1) // spread
    indices = jnp.arange(held, dtype=jnp.int32)
    matched = (owners[:, None] == owners[None, :]) & (indices[None, :] < indices[:, None])
    ranks = jnp.sum(matched.astype(jnp.int32), axis=1)
    positions = owners * capacity + ranks
    places = peers * capacity
    routing = jnp.arange(places, dtype=jnp.int32)[:, None] == positions[None, :]
    outgoing = jnp.dot(
        routing.astype(jnp.bfloat16), old_flat, preferred_element_type=jnp.float32
    ).astype(jnp.bfloat16)
    labels = jnp.sum(jnp.where(routing, slots[None, :] + 1, 0), axis=1) - 1
    arrived, arrived_tags = (
        lax.all_to_all(outgoing, ROW_COL, split_axis=0, concat_axis=0, tiled=True),
        lax.all_to_all(labels, ROW_COL, split_axis=0, concat_axis=0, tiled=True),
    )
    slots_here = per_row * per_col
    collect = (jnp.arange(slots_here, dtype=jnp.int32)[:, None] == arrived_tags[None, :]).astype(
        jnp.bfloat16
    )
    summed = jnp.dot(collect, arrived, preferred_element_type=jnp.float32)
    front_c = (
        summed.reshape(per_row, per_col, tile_side, tile_side)
        .transpose(0, 2, 1, 3)
        .reshape(row_span, col_span)
    )
    orders = pivot_order[0]
    coeff_one = make_coeffs(block_inverses[0, 0], pivot_pattern[0, 0], delays[0, 0], panel)
    coeff_two = make_coeffs(block_inverses[0, 1], pivot_pattern[0, 1], delays[0, 1], panel)
    own_rows = pivot_cols[0]
    own_first = jnp.take(own_rows[:, :panel], orders[0], axis=1)
    own_second_raw = jnp.take(own_rows[:, panel:], orders[1], axis=1)
    own_start = (row_index * col_devices + col_index) * rows_here
    both_panels = gather_axes(
        jnp.concatenate([own_first, own_second_raw], axis=1), ROW_COL, (0, 2, 1), 0
    )
    first = both_panels[:, :panel].astype(jnp.float32)
    picked = jnp.take(first, panel + orders[1], axis=0)
    second = both_panels[:, panel:].astype(jnp.float32) - outer_update(
        scale_pivots(first, coeff_one), picked
    )
    own_second = lax.dynamic_slice_in_dim(second, own_start, rows_here, 0)
    pivot_span = 2 * panel
    row_first = scale_pivots(
        lax.dynamic_slice_in_dim(first, pivot_span + row_index * row_span, row_span, 0), coeff_one
    )
    row_second = scale_pivots(
        lax.dynamic_slice_in_dim(second, pivot_span + row_index * row_span, row_span, 0), coeff_two
    )
    col_first = lax.dynamic_slice_in_dim(first, pivot_span + col_index * col_span, col_span, 0)
    col_second = lax.dynamic_slice_in_dim(second, pivot_span + col_index * col_span, col_span, 0)
    parent = summed_on_arrival(
        front_c - outer_update(row_first, col_first) - outer_update(row_second, col_second),
        "team",
        0,
    )
    return (parent[None], own_second[None])


def solution(mesh):
    torus = Mesh(
        mesh.devices.reshape(mesh.shape["team"], mesh.shape["row"], 4, 4),
        ("team", "row", "col_0", "col_1"),
    )
    in_specs = (
        P("team", ROW_COL, None, None),
        P("team", ROW_COL),
        P("team", ROW_COL, None),
        P("team", None, None),
        P("team", None, None),
        P("team", None, None, None),
        P("team", None),
    )
    out_specs = (P("row", "team", COL), P("team", ROW_COL, None))
    return jax.shard_map(local, mesh=torus, in_specs=in_specs, out_specs=out_specs, check_vma=False)
```

profile of v0, /device:TPU:38, one launch (start us, length us, event | category | flops | bytes accessed | tf_op | source)
XLA Modules:
  0.0 434.8 jit_solution(3782700567953836906)
XLA Ops:
  9.3 2.6 gather_fusion.2
  13.8 2.6 gather_fusion.1
  19.3 1.9 copy.19
  21.2 23.7 %all-gather = bf16[320,1024]{1,0:T(8,128)(2,1)} all-gather(bf16[160,1024]{1,0:T(8,128)(2,1)} %copy.19), channel_id=2, replica_groups=mesh['team'=8,'row'=2,'col_0'=4,'col_1'=4] {'row'}, dimensions={0}, use_global_device_ids=true | all-gather | bytes 983040 | tf_op jit(solution)/shard_map/all_gather | solution.py:20
  46.0 8.6 %all-to-all-start = ((s32[32,2,1]{1,2,0:T(1,128)}), s32[32,2,1]{1,2,0:T(1,128)S(1)}, u32[]{:S(2)}, u32[]{:S(2)}) async-start(s32[32,2,1]{1,2,0:T(1,128)} %bitcast.5), calls=%async_computation | async-start | bytes 32768 | tf_op jit(solution)/shard_map/all_to_all | solution.py:115
  56.4 5.7 %convolution_convert_fusion = bf16[64,65536]{1,0:T(8,128)(2,1)} fusion(bf16[24,65536]{1,0:T(8,128)(2,1)S(1)} %bitcast.64, s32[24]{0:T(128)S(1)} %fusion.37), kind=kOutput, calls=%fused_computation.3 | convolution fusion | flops 205522432 | bytes 11534432 | tf_op jit(solution)/shard_map/dot_general | solution.py:109
  62.2 10.6 %all_to_all.16 = bf16[32,2,65536]{2,1,0:T(2,128)(2,1)} reshape(bf16[64,65536]{1,0:T(8,128)(2,1)} %convolution_convert_fusion) | data formatting | bytes 16777216 | tf_op jit(solution)/shard_map/all_to_all | solution.py:114
  72.8 10.0 %all-to-all-start.1 = ((bf16[32,2,65536]{2,1,0:T(2,128)(2,1)}), bf16[32,2,65536]{2,1,0:T(2,128)(2,1)}, u32[]{:S(2)}, u32[]{:S(2)}) async-start(bf16[32,2,65536]{2,1,0:T(2,128)(2,1)} %all_to_all.16), calls=%async_computation.1 | async-start | bytes 16777216 | tf_op jit(solution)/shard_map/all_to_all | solution.py:114
  83.0 89.3 %all-gather.4.cloned.1.call-done = bf16[8,160,1024]{2,1,0:T(8,128)(2,1)} async-done(((bf16[2,160,1024]{2,1,0:T(8,128)(2,1)}), bf16[8,160,1024]{2,1,0:T(8,128)(2,1)}) %all-gather.4.cloned.1.call-update) | async-done | bytes 2621456 | tf_op jit(solution)/shard_map/all_gather | solution.py:20
  175.7 114.1 %all-to-all-done.1 = bf16[32,2,65536]{2,1,0:T(2,128)(2,1)} async-done(((bf16[32,2,65536]{2,1,0:T(2,128)(2,1)}), bf16[32,2,65536]{2,1,0:T(2,128)(2,1)}, u32[]{:S(2)}, u32[]{:S(2)}) %all-to-all-start.1) | async-done | bytes 8388640 | tf_op jit(solution)/shard_map/all_to_all | solution.py:114
  289.8 10.2 %all_to_all.18 = bf16[64,65536]{1,0:T(8,128)(2,1)} reshape(bf16[32,2,65536]{2,1,0:T(2,128)(2,1)} %all-to-all-done.1) | data formatting | bytes 16777216 | tf_op jit(solution)/shard_map/all_to_all | solution.py:114
  300.0 4.6 %fusion.27 = f32[8,65536]{1,0:T(8,128)S(1)} fusion(bf16[64,65536]{1,0:T(8,128)(2,1)} %all_to_all.18, s32[64]{0:T(128)S(1)} %eq.58), kind=kOutput, calls=%fused_computation.48 | convolution fusion | flops 67109376 | bytes 10486016 | tf_op jit(solution)/shard_map/dot_general | solution.py:121
  306.2 20.3 %all-gather.6.cloned.1.call-done = bf16[32,160,1024]{2,1,0:T(8,128)(2,1)} async-done(((bf16[8,160,1024]{2,1,0:T(8,128)(2,1)}), bf16[32,160,1024]{2,1,0:T(8,128)(2,1)}) %all-gather.6.cloned.1.call-update) | async-done | bytes 10485776 | tf_op jit(solution)/shard_map/all_gather | solution.py:20
  326.5 9.8 %copy.20 = bf16[2,4,4,160,1024]{4,3,2,1,0:T(8,128)(2,1)} copy(bf16[2,4,4,160,1024]{4,3,0,2,1:T(8,128)(2,1)} %bitcast.65) | data formatting | bytes 20971520 | tf_op jit(solution)/shard_map/transpose | solution.py:24
  336.4 10.0 %fusion.42 = (bf16[5120,512]{1,0:T(8,128)(2,1)}, f32[5120,512]{1,0:T(8,128)}) fusion(bf16[5120,1024]{1,0:T(8,128)(2,1)} %bitcast.60), kind=kLoop, calls=%fused_computation.99 | loop fusion | flops 2621440 | bytes 20971520 | tf_op jit(solution)/shard_map/slice | solution.py:137
  346.3 6.2 %gather_fusion = f32[512,512]{1,0:T(8,128)S(1)} fusion(f32[5120,512]{1,0:T(8,128)} %get-tuple-element.12, s32[1024]{0:T(1024)S(1)} %pad_clamp_fusion), kind=kCustom, calls=%fused_computation.2 | custom fusion | bytes 2099200 | tf_op jit(solution)/shard_map/jit(_take)/gather | solution.py:138
  352.5 9.2 %multiply_add_fusion.1 = (f32[5120,256]{1,0:T(8,128)}, f32[5120,256]{1,0:T(8,128)}) fusion(f32[5120,512]{1,0:T(8,128)} %get-tuple-element.12, f32[256]{0:T(256)S(1)} %get-tuple-element.32, f32[256]{0:T(256)S(1)} %get-tuple-element.30, f32[256]{0:T(256)S(1)} %get-tuple-element.31), kind=kLoop, calls=%fused_computation.10 | loop fusion | flops 7864320 | bytes 20974592 | tf_op jit(solution)/shard_map/add | solution.py:61
  361.7 2.8 multiply_add_fusion.5
  365.4 20.4 %convert_subtract_fusion = f32[5120,512]{1,0:T(8,128)S(1)} fusion(f32[5120,256]{1,0:T(8,128)} %get-tuple-element.8, f32[5120,256]{1,0:T(8,128)S(1)} %copy-done.1, bf16[5120,1024]{1,0:T(8,128)(2,1)S(1)} %bitcast.63, f32[512,512]{1,0:T(8,128)S(1)} %gather_fusion, pred[512]{0:T(512)(128)(4,1)S(1)} %get-tuple-element.28), kind=kOutput, calls=%fused_computation.8 | convolution fusion | flops 16114253824 | bytes 27263488 | tf_op jit(solution)/shard_map/dot_general | solution.py:69
  386.4 2.6 copy-done.2
  389.0 3.4 fusion.17
  392.4 5.0 %fusion.14 = f32[2048,256]{1,0:T(8,128)} fusion(f32[2048,256]{1,0:T(8,128)S(1)} %fusion.17, f32[2048,256]{1,0:T(8,128)S(1)} %get-tuple-element.6, f32[2048,256]{1,0:T(8,128)S(1)} %get-tuple-element.5, f32[5120,512]{1,0:T(8,128)S(1)} %convert_subtract_fusion, s32[]{:T(128)S(6)} %select_n.109), kind=kOutput, calls=%fused_computation.19 | convolution fusion | flops 3222798336 | bytes 8912900 | tf_op jit(solution)/shard_map/dot_general | solution.py:69
  397.4 4.7 %all-to-all-start.2 = ((f32[8,256,256]{2,1,0:T(8,128)}), f32[8,256,256]{2,1,0:T(8,128)S(1)}, u32[]{:S(2)}, u32[]{:S(2)}) async-start(f32[8,256,256]{2,1,0:T(8,128)} %bitcast.28), calls=%async_computation.2 | async-start | bytes 4194304 | tf_op jit(solution)/shard_map/all_to_all | solution.py:38
  403.8 23.4 %all-to-all-done.2 = f32[8,256,256]{2,1,0:T(8,128)S(1)} async-done(((f32[8,256,256]{2,1,0:T(8,128)}), f32[8,256,256]{2,1,0:T(8,128)S(1)}, u32[]{:S(2)}, u32[]{:S(2)}) %all-to-all-start.2) | async-done | bytes 2097184 | tf_op jit(solution)/shard_map/all_to_all | solution.py:38
  (64 shorter events, 17.6 us)
Async XLA Ops:
  7.2 165.1 %all-gather.4.cloned.1.call-start = ((), (), s32[]{:S(2)}) async-start(), calls=%async_computation.3 | async-start | bytes 3276800 | tf_op jit(solution)/shard_map/all_gather | solution.py:20
  9.2 35.7 %copy-start.8 = (s32[1,24]{1,0:T(1,128)S(1)}, s32[1,24]{1,0:T(1,128)}, u32[]{:S(2)}) copy-start(s32[1,24]{1,0:T(1,128)} %param.10) | copy-start | bytes 292
  11.8 42.8 %copy-start.3 = (bf16[1,24,256,256]{3,2,1,0:T(8,128)(2,1)S(1)}, bf16[1,24,256,256]{3,2,1,0:T(8,128)(2,1)}, u32[]{:S(2)}) copy-start(bf16[1,24,256,256]{3,2,1,0:T(8,128)(2,1)} %param.9) | copy-start | bytes 9437188
  46.0 26.8 %all-to-all-start = ((s32[32,2,1]{1,2,0:T(1,128)}), s32[32,2,1]{1,2,0:T(1,128)S(1)}, u32[]{:S(2)}, u32[]{:S(2)}) async-start(s32[32,2,1]{1,2,0:T(1,128)} %bitcast.5), calls=%async_computation | async-start | bytes 32768 | tf_op jit(solution)/shard_map/all_to_all | solution.py:115
  72.8 99.6 %copy-start.7 = (s32[1,2]{1,0:T(1,128)S(1)}, s32[1,2]{1,0:T(1,128)}, u32[]{:S(2)}) copy-start(s32[1,2]{1,0:T(1,128)} %param.15) | copy-start | bytes 28
  72.8 101.5 %copy-start.4 = (s32[1,2,512]{2,1,0:T(2,128)S(1)}, s32[1,2,512]{2,1,0:T(2,128)}, u32[]{:S(2)}) copy-start(s32[1,2,512]{2,1,0:T(2,128)} %param.12) | copy-start | bytes 12292
  72.8 101.5 %copy-start.6 = (s32[1,2,256]{2,1,0:T(2,128)S(1)}, s32[1,2,256]{2,1,0:T(2,128)}, u32[]{:S(2)}) copy-start(s32[1,2,256]{2,1,0:T(2,128)} %param.13) | copy-start | bytes 6148
  72.8 101.5 %copy-start.5 = (f32[1,2,3,256]{3,1,2,0:T(2,128)S(1)}, f32[1,2,3,256]{3,1,2,0:T(2,128)}, u32[]{:S(2)}) copy-start(f32[1,2,3,256]{3,1,2,0:T(2,128)} %param.14) | copy-start | bytes 18436
  72.8 217.0 %all-to-all-start.1 = ((bf16[32,2,65536]{2,1,0:T(2,128)(2,1)}), bf16[32,2,65536]{2,1,0:T(2,128)(2,1)}, u32[]{:S(2)}, u32[]{:S(2)}) async-start(bf16[32,2,65536]{2,1,0:T(2,128)(2,1)} %all_to_all.16), calls=%async_computation.1 | async-start | bytes 16777216 | tf_op jit(solution)/shard_map/all_to_all | solution.py:114
  82.8 243.7 %all-gather.6.cloned.1.call-start = ((), (), s32[]{:S(2)}) async-start(), calls=%async_computation.4 | async-start | bytes 13107200 | tf_op jit(solution)/shard_map/all_gather | solution.py:20
  346.3 18.2 %slice-start = ((s8[10485760]{0:T(1024)(128)(4,1)}), s8[2097152]{0:T(1024)(128)(4,1)S(1)}, s32[]{:S(2)}) async-start(s8[10485760]{0:T(1024)(128)(4,1)} %bitcast.61), calls=%async_computation.5 | async-start | bytes 4194304
  352.5 12.0 %slice-start.1 = ((s8[10485760]{0:T(1024)(128)(4,1)}), s8[4194304]{0:T(1024)(128)(4,1)S(1)}, s32[]{:S(2)}) async-start(s8[10485760]{0:T(1024)(128)(4,1)} %bitcast.61), calls=%async_computation.6 | async-start | bytes 8388608
  352.5 12.0 %slice-start.2 = ((s8[10485760]{0:T(1024)(128)(4,1)}), s8[4194304]{0:T(1024)(128)(4,1)S(1)}, s32[]{:S(2)}) async-start(s8[10485760]{0:T(1024)(128)(4,1)} %bitcast.61), calls=%async_computation.7 | async-start | bytes 8388608
  361.7 3.7 copy-start.1
  385.8 6.6 %copy-start = (f32[5120,512]{1,0:T(8,128)}, f32[5120,512]{1,0:T(8,128)S(1)}, u32[]{:S(2)}) copy-start(f32[5120,512]{1,0:T(8,128)S(1)} %convert_subtract_fusion) | copy-start | bytes 31457284
  385.8 3.2 copy-start.2
  397.4 29.8 %all-to-all-start.2 = ((f32[8,256,256]{2,1,0:T(8,128)}), f32[8,256,256]{2,1,0:T(8,128)S(1)}, u32[]{:S(2)}, u32[]{:S(2)}) async-start(f32[8,256,256]{2,1,0:T(8,128)} %bitcast.28), calls=%async_computation.2 | async-start | bytes 4194304 | tf_op jit(solution)/shard_map/all_to_all | solution.py:38
Sparse Core Ops, SparseCore 0:
  45.0 127.1 all-gather.3
  174.1 152.3 all-gather.5
where the time goes:
time: 440 us; the launch traced here: 435 us
  waiting for transfers between devices  247 us (56%)
  local copies, waits for them, and re-layouts  56.5 us (13%)
  matrix products  39.1 us (9%)
  other arithmetic  29.3 us (7%)
  blocking collectives  23.7 us (5%)
  starting transfers between devices  23.5 us (5%)
  between operations  15.7 us (4%)
    all_to_all x1, waiting for transfers between devices, local(): lax.all_to_all(outgoing, ROW_COL, split_axis=0, concat_axis=0, tiled=True)  114 us
    all_gather x2, waiting for transfers between devices, all_blocks(): pieces = lax.all_gather(pieces, axes[k], axis=0, tiled=True)  110 us
    dot_general x3, matrix products, outer_update(): lax.dot_general(left_rows, right_rows, (((1,), (1,)), ((), ())), precisio...  28.8 us
    all_gather x1, blocking collectives, all_blocks(): pieces = lax.all_gather(pieces, axes[k], axis=0, tiled=True)  23.7 us
    all_to_all x1, waiting for transfers between devices, summed_on_arrival(): lax.all_to_all(pieces, axis, split_axis=0, concat_axis=0, tiled=True)  23.4 us
    all_to_all x2, local copies, waits for them, and re-layouts, local(): lax.all_to_all(outgoing, ROW_COL, split_axis=0, concat_axis=0, tiled=True)  20.8 us
    add x3, other arithmetic, scale_pivots(): left_half * diag_one + right_half * off_diag  12.5 us
    all_to_all x1, starting transfers between devices, local(): lax.all_to_all(outgoing, ROW_COL, split_axis=0, concat_axis=0, tiled=True)  10 us
  transfers between devices with their start and end apart: 5, of which 4 were waited for; matrix products, arithmetic and copies ran while one was open for 4% of the time, Pallas kernels for 0%

commit v1 on v0

v1 whole, which is shorter than its diff:
```python
import jax
import jax.numpy as jnp
from jax import lax
from jax.experimental import pallas as pl
from jax.experimental.pallas import tpu as pltpu
from jax.sharding import Mesh
from jax.sharding import PartitionSpec as P

AXES = ("x", "core", "zh", "y", "zl")
ID = pl.DeviceIdType.MESH
HALF = 256
PANEL = 512
TILE = 256
SHARD = 160
PIVOTS = 1024
F32 = jnp.float32
BF16 = jnp.bfloat16
VMEM = pl.BlockSpec(memory_space=pltpu.VMEM)


def place():
    x = lax.axis_index("x")
    core = lax.axis_index("core")
    z = lax.axis_index("zh") * 4 + lax.axis_index("zl")
    y = lax.axis_index("y")
    return x, core, y, z


def device(x, core, y, z):
    return {"x": x, "core": core, "zh": z // 4, "y": y, "zl": z % 4}


def plane_peers(x, core, y):
    peers = []
    for dx in range(4):
        for dy in range(4):
            for dc in range(2):
                if dx or dy or dc:
                    peers.append(((x + dx) % 4, (core + dc) % 2, (y + dy) % 4))
    return peers


def line_peers(x, core, y, z):
    peers = []
    for dx in range(4):
        for dc in range(2):
            if dx or dc:
                peers.append((0, device((x + dx) % 4, (core + dc) % 2, y, z)))
    for dy in range(1, 4):
        peers.append((1, device(x, core, (y + dy) % 4, z)))
    for dz in range(1, 8):
        peers.append((2, device(x, core, y, (z + dz) % 8)))
    return peers


def enter_all(x, core, y, z, gate):
    barrier = pltpu.get_barrier_semaphore()
    peers = line_peers(x, core, y, z)
    for _, peer in peers:
        pl.semaphore_signal(barrier, inc=1, device_id=peer, device_id_type=ID)
    pl.semaphore_wait(barrier, len(peers))
    for axis in (1, 2):
        group = [peer for kind, peer in peers if kind == axis]
        for peer in group:
            pl.semaphore_signal(gate.at[axis - 1], inc=1, device_id=peer, device_id_type=ID)
        pl.semaphore_wait(gate.at[axis - 1], len(group))


def send(src, dst, send_sem, recv_sem, peer):
    copy = pltpu.make_async_remote_copy(
        src_ref=src, dst_ref=dst, send_sem=send_sem, recv_sem=recv_sem, device_id=peer, device_id_type=ID
    )
    copy.start()
    return copy


def wait_bytes(ref, sem):
    pltpu.make_async_copy(ref, ref, sem).wait()


def exchange_kernel(
    tiles, tags, shard, zrows, yrows, grows, trecv, tagrecv,
    zu_s, zu_r, zd_s, zd_r, y_s, y_r, gu_s, gu_r, gd_s, gd_r, t_s, t_r, gate,
):
    x, core, y, z = place()
    enter_all(x, core, y, z, gate)
    up = device(x, core, y, (z + 1) % 8)
    down = device(x, core, y, (z + 7) % 8)
    right = device(x, core, (y + 1) % 4, z)
    left = device(x, core, (y + 3) % 4, z)
    mine = (x * 2 + core) * 4 + y
    half = SHARD // 2
    sent = []
    sent.append(send(shard, yrows.at[y], y_s.at[0], y_r.at[0], right))
    sent.append(send(shard, yrows.at[y], y_s.at[1], y_r.at[1], left))
    sent.append(send(shard, zrows.at[z], zu_s.at[0], zu_r.at[0], up))
    sent.append(send(shard, zrows.at[z], zd_s.at[0], zd_r.at[0], down))
    for px, pc, py in plane_peers(x, core, y):
        other = (px * 2 + pc) * 4 + py
        peer = device(px, pc, py, z)
        send(tags, tagrecv.at[mine], t_s.at[1], t_r.at[1], peer)
        send(tiles.at[:, pl.ds(pl.multiple_of(other * 8, 8), 8), :], trecv.at[mine], t_s.at[0], t_r.at[0], peer)
    zrows[z] = shard[...]
    yrows[y] = shard[...]
    tagrecv[mine] = tags[...]
    trecv[mine] = tiles[:, pl.ds(pl.multiple_of(mine * 8, 8), 8), :]

    def land(ref, sem):
        wait_bytes(ref, sem)

    y_left = (y + 3) % 4
    y_right = (y + 1) % 4
    land(yrows.at[y_left], y_r.at[0])
    part = yrows.at[y_left, 0:half]
    sent.append(send(part, part, y_s.at[2], y_r.at[2], right))
    land(yrows.at[y_right], y_r.at[1])
    part = yrows.at[y_right, half:SHARD]
    sent.append(send(part, part, y_s.at[3], y_r.at[3], left))
    for step in range(2, 5):
        src = (z + 9 - step) % 8
        land(zrows.at[src], zu_r.at[step - 2])
        part = zrows.at[src] if step < 4 else zrows.at[src, 0:half]
        sent.append(send(part, part, zu_s.at[step - 1], zu_r.at[step - 1], up))
        src = (z + step - 1) % 8
        land(zrows.at[src], zd_r.at[step - 2])
        part = zrows.at[src] if step < 4 else zrows.at[src, half:SHARD]
        sent.append(send(part, part, zd_s.at[step - 1], zd_r.at[step - 1], down))
        if step == 2:
            opposite = (y + 2) % 4
            land(yrows.at[opposite, 0:half], y_r.at[2])
            land(yrows.at[opposite, half:SHARD], y_r.at[3])
            pivot_y = jnp.where(z == 3, 0, 1)

            @pl.when(z < 4)
            def _():
                grows[z] = yrows[pivot_y, :, 0:PANEL]
                first = yrows.at[pivot_y, :, 0:PANEL]
                send(first, grows.at[z], gu_s.at[0], gu_r.at[0], up)
                send(first, grows.at[z], gd_s.at[0], gd_r.at[0], down)

    for step in range(2, 5):
        src = (z + 9 - step) % 8

        @pl.when(src < 4)
        def _(step=step, src=src):
            land(grows.at[src], gu_r.at[step - 2])
            send(grows.at[src], grows.at[src], gu_s.at[step - 1], gu_r.at[step - 1], up)

        src = (z + step - 1) % 8

        @pl.when(src < 4)
        def _(step=step, src=src):
            land(grows.at[src], gd_r.at[step - 2])
            if step < 4:
                send(grows.at[src], grows.at[src], gd_s.at[step - 1], gd_r.at[step - 1], down)

    @pl.when((z + 4) % 8 < 4)
    def _():
        land(grows.at[(z + 4) % 8], gu_r.at[3])

    land(zrows.at[(z + 4) % 8, 0:half], zu_r.at[3])
    land(zrows.at[(z + 4) % 8, half:SHARD], zd_r.at[3])
    land(trecv.at[0:31], t_r.at[0])
    land(tagrecv.at[0:31], t_r.at[1])
    wait_bytes(trecv.at[0:31], t_s.at[0])
    wait_bytes(tagrecv.at[0:31], t_s.at[1])
    for copy in sent:
        copy.wait_send()
    for step in range(1, 5):
        src = (z + 9 - step) % 8

        @pl.when(src < 4)
        def _(step=step, src=src):
            wait_bytes(grows.at[src], gu_s.at[step - 1])

        if step < 4:
            src = (z + step - 1) % 8

            @pl.when(src < 4)
            def _(step=step, src=src):
                wait_bytes(grows.at[src], gd_s.at[step - 1])


def exchange(tiles, tags, shard):
    held = tiles.shape[0]
    dma = pltpu.SemaphoreType.DMA
    return pl.pallas_call(
        exchange_kernel,
        out_shape=(
            jax.ShapeDtypeStruct((8, SHARD, 2 * PANEL), BF16),
            jax.ShapeDtypeStruct((4, SHARD, 2 * PANEL), BF16),
            jax.ShapeDtypeStruct((4, SHARD, PANEL), BF16),
            jax.ShapeDtypeStruct((32, held, 8, TILE), BF16),
            jax.ShapeDtypeStruct((32, 8, 128), jnp.int32),
        ),
        in_specs=[VMEM] * 3,
        out_specs=(VMEM,) * 5,
        scratch_shapes=[
            dma((4,)), dma((4,)), dma((4,)), dma((4,)), dma((4,)), dma((4,)),
            dma((4,)), dma((4,)), dma((3,)), dma((3,)), dma((2,)), dma((2,)),
            pltpu.SemaphoreType.REGULAR((2,)),
        ],
        compiler_params=pltpu.CompilerParams(collective_id=0, has_side_effects=True),
        name="exchange",
    )(tiles, tags, shard)


def scatter_kernel(index, slices, out):
    out[...] = jnp.zeros_like(out)

    @pl.loop(0, slices.shape[0], unroll=8)
    def _(k):
        out[index[k]] += slices[k].astype(F32)


def scatter(index, slices):
    return pl.pallas_call(
        scatter_kernel,
        out_shape=jax.ShapeDtypeStruct((256, 8, TILE), F32),
        in_specs=[pl.BlockSpec(memory_space=pltpu.SMEM), VMEM],
        out_specs=VMEM,
        name="scatter",
    )(index, slices)


def reduce_kernel(
    update, sums, piece, ring, cores, keep, across, up_send, up_recv, dn_send, dn_recv,
    c_s, c_r, x_s, x_r, u_s, u_r, d_s, d_r, gate,
):
    x, core, y, z = place()
    enter_all(x, core, y, z, gate)
    up = device(x, core, y, (z + 1) % 8)
    down = device(x, core, y, (z + 7) % 8)
    width = 4 * SHARD
    other = 1 - core
    sent = [
        send(
            update.at[:, pl.ds(pl.multiple_of(other * width, 128), width)],
            cores, c_s.at[0], c_r.at[0], device(x, other, y, z),
        ),
        send(sums.at[(z + 4) % 8], up_recv.at[0], u_s.at[0], u_r.at[0], up),
        send(sums.at[(z + 5) % 8], dn_recv.at[0], d_s.at[0], d_r.at[0], down),
    ]
    wait_bytes(cores, c_r.at[0])
    keep[...] = update[:, pl.ds(pl.multiple_of(core * width, 128), width)] + cores[...]
    for dx in (1, 3, 2):
        px = (x + dx) % 4
        sent.append(
            send(
                keep.at[pl.ds(pl.multiple_of(px * SHARD, 8), SHARD)],
                across.at[3 - dx], x_s.at[dx - 1], x_r.at[3 - dx], device(px, core, y, z),
            )
        )
    for step in range(1, 4):
        wait_bytes(up_recv.at[step - 1], u_r.at[step - 1])
        up_send[step - 1] = up_recv[step - 1] + sums[(z + 4 - step) % 8]
        sent.append(send(up_send.at[step - 1], up_recv.at[step], u_s.at[step], u_r.at[step], up))
        if step < 3:
            wait_bytes(dn_recv.at[step - 1], d_r.at[step - 1])
            dn_send[step - 1] = dn_recv[step - 1] + sums[(z + 5 + step) % 8]
            sent.append(send(dn_send.at[step - 1], dn_recv.at[step], d_s.at[step], d_r.at[step], down))
    for slot in range(3):
        wait_bytes(across.at[slot], x_r.at[slot])
    piece[...] = (
        keep[pl.ds(pl.multiple_of(x * SHARD, 8), SHARD)] + across[0] + across[1] + across[2]
    )
    wait_bytes(up_recv.at[3], u_r.at[3])
    wait_bytes(dn_recv.at[2], d_r.at[2])
    ring[...] = sums[z] + up_recv[3] + dn_recv[2]
    for copy in sent:
        copy.wait_send()


def reduce_both(update, sums):
    dma = pltpu.SemaphoreType.DMA
    block = (32, 8, TILE)
    return pl.pallas_call(
        reduce_kernel,
        out_shape=(
            jax.ShapeDtypeStruct((SHARD, 4 * SHARD), F32),
            jax.ShapeDtypeStruct(block, F32),
        ),
        in_specs=[VMEM] * 2,
        out_specs=(VMEM,) * 2,
        scratch_shapes=[
            pltpu.VMEM((4 * SHARD, 4 * SHARD), F32),
            pltpu.VMEM((4 * SHARD, 4 * SHARD), F32),
            pltpu.VMEM((3, SHARD, 4 * SHARD), F32),
            pltpu.VMEM((3, *block), F32),
            pltpu.VMEM((4, *block), F32),
            pltpu.VMEM((2, *block), F32),
            pltpu.VMEM((3, *block), F32),
            dma((1,)), dma((1,)), dma((3,)), dma((3,)), dma((4,)), dma((4,)), dma((3,)), dma((3,)),
            pltpu.SemaphoreType.REGULAR((2,)),
        ],
        compiler_params=pltpu.CompilerParams(collective_id=1, has_side_effects=True),
        name="reduce_both",
    )(update, sums)


def deliver_kernel(piece, ring, parent, upd, tot, p_s, p_l, p_r, t_s, t_r, gate):
    x, core, y, z = place()
    enter_all(x, core, y, z, gate)
    row0 = (z // 4) * 2560 + x * 640 + (z % 4) * SHARD - PIVOTS
    col0 = core * 2560 + y * 640 - PIVOTS

    def each(action):
        for a in range(5):
            for b in range(5):
                row = row0 + 32 * a
                col = col0 + 128 * b
                i = row // TILE
                j = col // TILE
                px, pc, pz, py = (i % 8) // 2, i % 2, (i // 8) * 4 + j % 4, j // 4
                real = (row >= 0) & (col >= 0)
                own = (px == x) & (pc == core) & (pz == z) & (py == y)
                src = piece.at[32 * a : 32 * a + 32, 128 * b : 128 * b + 128]
                dst = upd.at[
                    pl.ds(pl.multiple_of(row % TILE, 32), 32), pl.ds(pl.multiple_of(col % TILE, 128), 128)
                ]
                action(real, own, src, dst, device(px, pc, py, pz), 5 * a + b)

    def start(real, own, src, dst, peer, n):
        @pl.when(real & jnp.logical_not(own))
        def _():
            send(src, dst, p_s.at[n], p_r.at[0], peer)

        @pl.when(real & own)
        def _():
            pltpu.make_async_copy(src, dst, p_r.at[0]).start()

    def finish(real, own, src, dst, peer, n):
        @pl.when(real & jnp.logical_not(own))
        def _():
            wait_bytes(src, p_s.at[n])

    each(start)
    mine = (x * 2 + core) * 4 + y
    for px, pc, py in plane_peers(x, core, y):
        other = (px * 2 + pc) * 4 + py
        send(
            ring.at[pc * 4 + py + px * 8],
            tot.at[mine], t_s.at[0], t_r.at[0], device(px, pc, py, z),
        )
    tot[mine] = ring[mine]
    wait_bytes(upd, p_r.at[0])
    wait_bytes(tot.at[0:31], t_r.at[0])
    wait_bytes(tot.at[0:31], t_s.at[0])
    for p in range(32):
        parent[8 * p : 8 * p + 8, :] = tot[p] - upd[8 * p : 8 * p + 8, :]
    each(finish)


def deliver(piece, ring):
    dma = pltpu.SemaphoreType.DMA
    return pl.pallas_call(
        deliver_kernel,
        out_shape=jax.ShapeDtypeStruct((TILE, TILE), F32),
        in_specs=[VMEM] * 2,
        out_specs=VMEM,
        scratch_shapes=[
            pltpu.VMEM((TILE, TILE), F32),
            pltpu.VMEM((32, 8, TILE), F32),
            dma((25,)), dma((1,)), dma((1,)), dma((1,)), dma((1,)),
            pltpu.SemaphoreType.REGULAR((2,)),
        ],
        compiler_params=pltpu.CompilerParams(collective_id=2, has_side_effects=True),
        name="deliver",
    )(piece, ring)


def split(v):
    hi = lax.reduce_precision(v, 8, 7)
    return hi.astype(BF16), (v - hi).astype(BF16)


def dot(a, b, dims):
    return lax.dot_general(a, b, (dims, ((), ())), preferred_element_type=F32)


def dot2(parts, b, dims):
    return dot(parts[0], b, dims) + dot(parts[1], b, dims)


def raw_coeffs(inverses, pattern, delay, order):
    positions = jnp.arange(PANEL, dtype=jnp.int32)
    active = (positions < PANEL - delay).astype(F32)
    lo, hi = active[:HALF], active[HALF:]
    da = inverses[0] * lo
    db = inverses[1] * pattern.astype(F32) * lo * hi
    dc = inverses[2] * hi
    diag = jnp.concatenate([da, dc])
    off = jnp.concatenate([db, db])
    partner = jnp.concatenate([order[HALF:], order[:HALF]])
    lanes = jnp.arange(PANEL, dtype=jnp.int32)
    here = order[:, None] == lanes[None, :]
    diag_raw = jnp.sum(jnp.where(here, diag[:, None], 0.0), axis=0)
    off_raw = jnp.sum(jnp.where(here, off[:, None], 0.0), axis=0)
    partner_raw = jnp.sum(jnp.where(here, partner[:, None], 0), axis=0)
    swap = (lanes[:, None] == partner_raw[None, :]).astype(BF16)
    return diag_raw, off_raw, swap


ROWS = ((1,), (1,))
COLS = ((1,), (0,))


def eliminate(zrows, yrows, grows, orders, pattern, inverses, delays, y):
    d1, o1, q1 = raw_coeffs(inverses[0], pattern[0], delays[0], orders[0])
    d2, o2, q2 = raw_coeffs(inverses[1], pattern[1], delays[1], orders[1])
    g = jnp.concatenate([grows[3, 32:], grows[0], grows[1], grows[2, :64]], axis=0)
    m1 = yrows[:, :, :PANEL].reshape(4 * SHARD, PANEL)
    m2 = yrows[:, :, PANEL:].reshape(4 * SHARD, PANEL)
    n1 = zrows[:, :, :PANEL].reshape(8 * SHARD, PANEL)
    n2 = zrows[:, :, PANEL:].reshape(8 * SHARD, PANEL)
    h1 = split(g.astype(F32) * d1 + dot(g, q1, COLS) * o1)
    second = m2.astype(F32) - (dot(m1, h1[0], ROWS) + dot(m1, h1[1], ROWS))
    y2 = second * d2 + dot2(split(second), q2, COLS) * o2
    y2s = split(y2)
    back = m1.astype(F32) - dot2(y2s, g, COLS)
    w1 = back * d1 + dot2(split(back), q1, COLS) * o1
    update = dot2(split(w1), n1, ROWS) + dot2(y2s, n2, ROWS)
    own = lax.dynamic_slice_in_dim(second, y * SHARD, SHARD, 0)
    perm = (jnp.arange(PANEL, dtype=jnp.int32)[:, None] == orders[1][None, :]).astype(BF16)
    return update, dot2(split(own), perm, COLS)


def local(old_tiles, remap, pivot_cols, pivot_order, pivot_pattern, block_inverses, delays):
    y = lax.axis_index("y")
    held = old_tiles.shape[1]
    tags = jnp.zeros((8, 128), jnp.int32).at[0, :held].set(remap[0])
    zrows, yrows, grows, trecv, tagrecv = exchange(old_tiles[0], tags, pivot_cols[0])
    target = tagrecv[:, 0, :held].reshape(-1)
    i, j = target // 16, target % 16
    index = ((i // 8) * 4 + j % 4) * 32 + (i % 8) * 4 + j // 4
    sums = scatter(index, trecv.reshape(32 * held, 8, TILE))
    update, second = eliminate(
        zrows, yrows, grows, pivot_order[0], pivot_pattern[0], block_inverses[0], delays[0], y
    )
    piece, ring = reduce_both(update, sums.reshape(8, 32, 8, TILE))
    parent = deliver(piece, ring)
    return parent[None], second[None]


def solution(mesh):
    grid = Mesh(mesh.devices.reshape(4, 2, 2, 4, 4), AXES)
    team, row_col = ("x", "core"), ("zh", "y", "zl")
    in_specs = (
        P(team, row_col, None, None),
        P(team, row_col),
        P(team, row_col, None),
        P(team, None, None),
        P(team, None, None),
        P(team, None, None, None),
        P(team, None),
    )
    out_specs = (P("zh", team, ("y", "zl")), P(team, row_col, None))
    return jax.shard_map(local, mesh=grid, in_specs=in_specs, out_specs=out_specs, check_vma=False)
```

time: 440 us -> 195 us (0.44); the launches traced: 435 us -> 195 us
  waiting for transfers between devices: 247 us -> 0 us
  Pallas kernels: 0 us -> 167 us
  local copies, waits for them, and re-layouts: 56.5 us -> 10.5 us
  other arithmetic: 29.3 us -> 2.44 us
  matrix products: 39.1 us -> 12.3 us
  blocking collectives: 23.7 us -> 0 us
  starting transfers between devices: 23.5 us -> 0 us
  between operations: 15.7 us -> 2.17 us
    pallas_call x0 -> x4, Pallas kernels: none -> 167 us  [the longest x1 84.9 us: exchange(): pl.pallas_call(exchange_kernel, out_shape=(jax.ShapeDtypeStruct((8, SHARD...]
    all_to_all x3 -> x0, waiting for transfers between devices: 138 us -> none  [the longest x1 114 us: local(): lax.all_to_all(outgoing, ROW_COL, split_axis=0, concat_axis=0, tiled=True)]
    all_gather x2 -> x0, waiting for transfers between devices: 110 us -> none  [all_blocks(): pieces = lax.all_gather(pieces, axes[k], axis=0, tiled=True)]
    dot_general x5 -> x15, matrix products: 39.1 us -> 12.3 us  [dot(): return lax.dot_general(a, b, (dims, ((), ())), preferred_element_type=F32)]
    all_gather x1 -> x0, blocking collectives: 23.7 us -> none  [all_blocks(): pieces = lax.all_gather(pieces, axes[k], axis=0, tiled=True)]
    all_to_all x3 -> x0, starting transfers between devices: 23.3 us -> none  [the longest x1 10 us: local(): lax.all_to_all(outgoing, ROW_COL, split_axis=0, concat_axis=0, tiled=True)]
    all_to_all x3 -> x0, local copies, waits for them, and re-layouts: 21.4 us -> none  [the longest x2 20.8 us: local(): lax.all_to_all(outgoing, ROW_COL, split_axis=0, concat_axis=0, tiled=True)]
    add x5 -> x1, other arithmetic: 12.6 us -> 0.62 us  [local(): index = (i // 8 * 4 + j % 4) * 32 + i % 8 * 4 + j // 4]
  transfers between devices with their start and end apart: 5 -> 0, of which waited for: 4 -> 0; matrix products, arithmetic and copies ran while one was open for 4% -> 0% of each run, Pallas kernels for 0% -> 0%
where the time goes in v1:
time: 195 us
  Pallas kernels  167 us (86%)
  matrix products  12.3 us (6%)
  local copies, waits for them, and re-layouts  10.5 us (5%)
  other arithmetic  2.44 us (1%)
  between operations  2.17 us (1%)
    pallas_call x1, Pallas kernels, exchange(): pl.pallas_call(exchange_kernel, out_shape=(jax.ShapeDtypeStruct((8, SHARD...  84.9 us
    pallas_call x1, Pallas kernels, reduce_both(): pl.pallas_call(reduce_kernel, out_shape=(jax.ShapeDtypeStruct((SHARD, 4 *...  43.7 us
    pallas_call x1, Pallas kernels, deliver(): pl.pallas_call(deliver_kernel, out_shape=jax.ShapeDtypeStruct((TILE, TILE...  33.1 us
    dot_general x15, matrix products, dot(): return lax.dot_general(a, b, (dims, ((), ())), preferred_element_type=F32)  12.3 us
    pallas_call x1, Pallas kernels, scatter(): pl.pallas_call(scatter_kernel, out_shape=jax.ShapeDtypeStruct((256, 8, TI...  5.69 us

profile of v1, /device:TPU:38, one launch (start us, length us, event | category | flops | bytes accessed | tf_op | source)
XLA Modules:
  0.0 194.8 jit_solution(10745742103811624918)
XLA Ops:
  0.6 1.3 fusion.61
  3.3 0.8 slice_convert_fusion
  4.0 1.3 scatter.6.tags
  5.3 0.8 fusion.60
  6.1 0.8 fusion.59
  7.3 0.8 fusion.58
  8.7 84.9 %exchange.1 = (bf16[8,160,1024]{2,1,0:T(8,128)(2,1)}, bf16[4,160,1024]{2,1,0:T(8,128)(2,1)}, bf16[4,160,512]{2,1,0:T(8,128)(2,1)}, bf16[32,24,8,256]{3,2,1,0:T(8,128)(2,1)}, s32[32,8,128]{2,1,0:T(8,128)}) custom-call(bf16[24,256,256]{2,1,0:T(8,128)(2,1)} %bitcast.51, s32[8,128]{1,0:T(8,128)} %scatter.6.tags, bf16[160,1024]{1,0:T(8,128)(2,1)} %bitcast.54), custom_call_target="tpu_custom_call" | custom-call | tf_op jit(solution)/shard_map/exchange/pallas_call | solution.py:187
  93.6 1.4 fusion.57
  95.0 0.9 slice_reduce_fusion
  96.1 0.6 fusion.40.index
  96.7 5.7 %scatter.7 = f32[256,8,256]{2,1,0:T(8,128)} custom-call(s32[768]{0:T(1024)} %fusion.40.index, bf16[768,8,256]{2,1,0:T(8,128)(2,1)} %bitcast.50), custom_call_target="tpu_custom_call" | custom-call | tf_op jit(solution)/shard_map/scatter/pallas_call | solution.py:217
  103.5 0.6 fusion.6
  104.4 1.1 fusion.12
  106.0 0.6 fusion.4
  107.7 0.6 fusion.16
  108.3 0.6 fusion.2
  108.8 1.1 copy-done
  110.3 1.1 fusion.31
  111.3 1.1 convolution_add_fusion
  112.4 1.1 fusion.20
  113.5 2.8 %fusion.update = f32[640,1280]{1,0:T(8,128)} fusion(f32[640,1280]{1,0:T(8,128)S(1)} %convolution_add_fusion, f32[640,1280]{1,0:T(8,128)S(1)} %fusion.20, bf16[1280,512]{1,0:T(8,128)(2,1)S(1)} %bitcast.43, f32[640,512]{1,0:T(8,128)S(1)} %fusion.2), kind=kOutput, calls=%fused_computation.2 | convolution fusion | flops 841482240 | bytes 12451840 | tf_op jit(solution)/shard_map/dot_general | solution.py:378
  116.3 43.7 %reduce_both.1 = (f32[160,640]{1,0:T(8,128)}, f32[32,8,256]{2,1,0:T(8,128)}) custom-call(f32[640,1280]{1,0:T(8,128)} %fusion.update, f32[8,32,8,256]{3,2,1,0:T(8,128)} %bitcast.49), custom_call_target="tpu_custom_call" | custom-call | tf_op jit(solution)/shard_map/reduce_both/pallas_call | solution.py:277
  160.0 33.1 %deliver.1 = f32[256,256]{1,0:T(8,128)} custom-call(f32[160,640]{1,0:T(8,128)} %get-tuple-element.26.piece, f32[32,8,256]{2,1,0:T(8,128)} %get-tuple-element.27.ring), custom_call_target="tpu_custom_call" | custom-call | tf_op jit(solution)/shard_map/deliver/pallas_call | solution.py:356
  193.1 1.7 copy.10
  (26 shorter events, 4.4 us)
Async XLA Ops:
  96.7 5.7 %copy-start.1 = (bf16[4,160,512]{2,1,0:T(8,128)(2,1)S(1)}, bf16[4,160,512]{2,1,0:T(8,128)(2,1)}, u32[]{:S(2)}) copy-start(bf16[4,160,512]{2,1,0:T(8,128)(2,1)} %get-tuple-element.22) | copy-start | bytes 1966084
  108.2 1.7 copy-start
